TPU v7x, 32 devices: a whole 2x2x4 slice. The times are simulated.
32 devices in a mesh: items: 8 (over z, y), users: 4 (over x, core).
Axes of the slice: x: 2, y: 2, z: 4, core: 2. Of those that a mesh axis runs over, the one named last changes fastest.
Arguments:
- user_emb: bfloat16 [4096, 256], P('users', 'items'), as said below
- item_emb: bfloat16 [262144, 256], P('items'), as said below
- target: int32 [4096], P('users'), may hold values from 0 to 262143
- history: int32 [4096, 32], P('users'), may hold values from 0 to 262143, as said below
Outputs:
- log_rank: float32 [4096], P('users')
- metrics: float32 [2], replicated
Inputs may be any that keep to these rules, and one draw needn't show every extreme that they name: history[u, k] lies in [k * 8192, (k + 1) * 8192); a user's history entries are thus distinct. `item_emb`: rows of norm about one. `user_emb`: entries of order one.
All inputs are finite; a program needn't handle non-finite values.
Results may differ from a plain program's by a relative error of at most 0.0003.
Values may be sent and summed in bfloat16 or wider, within the bound.
A program may use at most 64 MiB of HBM per device.

v0:
```python
import jax
import jax.numpy as jnp
from jax import lax
from jax.sharding import PartitionSpec as P

sharpness = 4.0


def body(user_emb, item_emb, target, history):
    item_dev = item_emb.shape[0]
    shard = lax.axis_index("items")
    start = shard * item_dev
    local_t = target - start
    inside = (local_t >= 0) & (local_t < item_dev)
    own_rows = item_emb[jnp.clip(local_t, 0, item_dev - 1)]
    users = lax.all_gather(user_emb, "items", axis=1, tiled=True)
    partial_t = jnp.sum(users.astype(jnp.float32) * own_rows.astype(jnp.float32), axis=1)
    tscore = lax.psum(jnp.where(inside, partial_t, 0.0), "items")
    n_items = lax.axis_size("items")
    n_users = lax.axis_size("users")
    u_dev = users.shape[0]
    blk = min(item_dev, 4096)
    nblk = item_dev // blk

    def add_block(index, total):
        rows = lax.dynamic_slice_in_dim(item_emb, index * blk, blk, 0)
        score = lax.dot_general(
            users, rows, (((1,), (1,)), ((), ())), preferred_element_type=jnp.float32
        )
        return total + jnp.sum(jax.nn.sigmoid(sharpness * (score - tscore[:, None])), axis=1)

    total = lax.fori_loop(0, nblk, add_block, jnp.zeros((u_dev,), jnp.float32))
    per_shard = history.shape[1] // n_items
    own_hist = lax.dynamic_slice_in_dim(history, shard * per_shard, per_shard, 1)
    hrows = item_emb[own_hist - start]
    hscore = jnp.einsum("ud,uhd->uh", users, hrows, preferred_element_type=jnp.float32)
    local = total - jnp.sum(jax.nn.sigmoid(sharpness * (hscore - tscore[:, None])), axis=1)
    seen = jnp.any(history == target[:, None], axis=1)
    correction = jnp.where(seen, 0.0, 0.5).astype(jnp.float32)
    all_users = u_dev * n_users
    above = lax.psum(local, "items") - correction
    rank = 1.0 + above
    log_rank = jnp.log(rank)
    hit = jax.nn.sigmoid(10.5 - rank)
    gain = hit / jnp.log2(1.0 + rank)
    hit_sum, gain_sum = lax.psum((jnp.sum(hit), jnp.sum(gain)), "users")
    metrics = jnp.stack([hit_sum, gain_sum]) / all_users
    return (log_rank, metrics)


def solution(mesh):
    return jax.shard_map(
        body,
        mesh=mesh,
        in_specs=(P("users", "items"), P("items", None), P("users"), P("users", None)),
        out_specs=(P("users"), P()),
        check_vma=False,
    )
```

profile of v0, /device:TPU:0, one launch (start us, length us, event | category | flops | bytes accessed | tf_op | source)
XLA Modules:
  0.0 174.1 jit_solution(5118468006411309888)
XLA Ops:
  0.7 0.8 compare_select_fusion
  1.5 0.2 copy.14
  1.7 0.3 reshape.17
  2.0 20.9 %gather_fusion.1 = bf16[4096,256]{1,0:T(8,128)(2,1)S(1)} fusion(bf16[32768,256]{1,0:T(8,128)(2,1)} %param.7, s32[4096]{0:T(1024)S(1)} %broadcast_clamp_fusion), kind=kCustom, calls=%fused_computation.1 | custom fusion | bytes 4210688 | tf_op jit(solution)/shard_map/gather | solution.py:35
  22.9 2.1 %reshape.16 = bf16[1024,4,256]{2,1,0:T(4,128)(2,1)} reshape(bf16[4096,256]{1,0:T(8,128)(2,1)S(1)} %gather_fusion.1) | data formatting | bytes 4194304 | tf_op jit(solution)/shard_map/gather | solution.py:35
  25.0 33.0 %all_gather.3 = bf16[1024,256]{0,1:T(8,128)(2,1)S(1)} all-gather(bf16[1024,32]{0,1:T(8,128)(2,1)S(1)} %copy-done.1), channel_id=1, replica_groups=mesh['items'=8,'users'=4] {'items'}, dimensions={1}, use_global_device_ids=true | all-gather | bytes 589824 | tf_op jit(solution)/shard_map/all_gather | solution.py:16
  58.2 2.9 %multiply_reduce_fusion = f32[1024,4]{1,0:T(8,128)S(1)} fusion(f32[1024,256]{1,0:T(8,128)S(1)} %copy.20, bf16[1024,4,256]{2,1,0:T(4,128)(2,1)} %reshape.16), kind=kLoop, calls=%fused_computation.7 | loop fusion | flops 3141632 | bytes 3162112
  61.3 11.4 %gather_fusion = bf16[1024,256]{1,0:T(8,128)(2,1)S(1)} fusion(bf16[32768,256]{1,0:T(8,128)(2,1)} %param.7, s32[1024]{0:T(1024)S(1)} %fusion.4), kind=kCustom, calls=%fused_computation | custom fusion | bytes 1052672 | tf_op jit(solution)/shard_map/gather | solution.py:15
  72.7 0.2 copy.13
  73.0 0.2 multiply_reduce_fusion.1
  73.2 21.5 %psum.28 = f32[1024]{0:T(1024)S(1)} all-reduce(f32[1024]{0:T(1024)S(1)} %and_select_fusion), channel_id=1, replica_groups=mesh['items'=8,'users'=4] {'items'}, use_global_device_ids=true, to_apply=%region_1.2 | all-reduce | flops 1024 | bytes 8192 | tf_op jit(solution)/shard_map/psum | solution.py:18
  94.8 52.7 %while.14 = (s32[]{:T(128)}, f32[1024]{0:T(1024)S(1)}, bf16[32768,256]{1,0:T(8,128)(2,1)}, bf16[1024,256]{1,0:T(8,128)(2,1)S(1)}, f32[1024]{0:T(1024)S(1)}, /*index=5*/s32[]{:T(128)}, s32[]{:T(128)}, s32[]{:T(128)}, s32[]{:T(128)}) while((s32[]{:T(128)}, f32[1024]{0:T(1024)S(1)}, bf16[32768,256]{1,0:T(8,128)(2,1)}, ...), condition=%wide.region_4.5_spmd.clone, body=%wide.region_2.4_spmd.clone.sunk | while | flops 2172650496 | bytes 2642073 | solution.py:32
  94.8 6.6 %fusion.11 = f32[1024]{0:T(1024)S(1)} fusion(bf16[1024,256]{1,0:T(8,128)(2,1)S(1)} %get-tuple-element.192, f32[1024]{0:T(1024)S(1)} %get-tuple-element.193, bf16[32768,256]{1,0:T(8,128)(2,1)} %get-tuple-element.191, s32[]{:T(128)S(6)} %select_n.43), kind=kOutput, calls=%fused_computation.3.clone.1 | convolution fusion | flops 2172648448 | bytes 2629636 | tf_op jit(solution)/shard_map/while/body/eval_jaxpr/dot_general | solution.py:27
  101.4 6.5 %fusion.11 = f32[1024]{0:T(1024)S(1)} fusion(bf16[1024,256]{1,0:T(8,128)(2,1)S(1)} %get-tuple-element.192, f32[1024]{0:T(1024)S(1)} %get-tuple-element.193, bf16[32768,256]{1,0:T(8,128)(2,1)} %get-tuple-element.191, s32[]{:T(128)S(6)} %select_n.43), kind=kOutput, calls=%fused_computation.3.clone.1 | convolution fusion | flops 2172648448 | bytes 2629636 | tf_op jit(solution)/shard_map/while/body/eval_jaxpr/dot_general | solution.py:27
  108.0 6.5 %fusion.11 = f32[1024]{0:T(1024)S(1)} fusion(bf16[1024,256]{1,0:T(8,128)(2,1)S(1)} %get-tuple-element.192, f32[1024]{0:T(1024)S(1)} %get-tuple-element.193, bf16[32768,256]{1,0:T(8,128)(2,1)} %get-tuple-element.191, s32[]{:T(128)S(6)} %select_n.43), kind=kOutput, calls=%fused_computation.3.clone.1 | convolution fusion | flops 2172648448 | bytes 2629636 | tf_op jit(solution)/shard_map/while/body/eval_jaxpr/dot_general | solution.py:27
  114.6 6.5 %fusion.11 = f32[1024]{0:T(1024)S(1)} fusion(bf16[1024,256]{1,0:T(8,128)(2,1)S(1)} %get-tuple-element.192, f32[1024]{0:T(1024)S(1)} %get-tuple-element.193, bf16[32768,256]{1,0:T(8,128)(2,1)} %get-tuple-element.191, s32[]{:T(128)S(6)} %select_n.43), kind=kOutput, calls=%fused_computation.3.clone.1 | convolution fusion | flops 2172648448 | bytes 2629636 | tf_op jit(solution)/shard_map/while/body/eval_jaxpr/dot_general | solution.py:27
  121.2 6.5 %fusion.11 = f32[1024]{0:T(1024)S(1)} fusion(bf16[1024,256]{1,0:T(8,128)(2,1)S(1)} %get-tuple-element.192, f32[1024]{0:T(1024)S(1)} %get-tuple-element.193, bf16[32768,256]{1,0:T(8,128)(2,1)} %get-tuple-element.191, s32[]{:T(128)S(6)} %select_n.43), kind=kOutput, calls=%fused_computation.3.clone.1 | convolution fusion | flops 2172648448 | bytes 2629636 | tf_op jit(solution)/shard_map/while/body/eval_jaxpr/dot_general | solution.py:27
  127.8 6.5 %fusion.11 = f32[1024]{0:T(1024)S(1)} fusion(bf16[1024,256]{1,0:T(8,128)(2,1)S(1)} %get-tuple-element.192, f32[1024]{0:T(1024)S(1)} %get-tuple-element.193, bf16[32768,256]{1,0:T(8,128)(2,1)} %get-tuple-element.191, s32[]{:T(128)S(6)} %select_n.43), kind=kOutput, calls=%fused_computation.3.clone.1 | convolution fusion | flops 2172648448 | bytes 2629636 | tf_op jit(solution)/shard_map/while/body/eval_jaxpr/dot_general | solution.py:27
  134.4 6.5 %fusion.11 = f32[1024]{0:T(1024)S(1)} fusion(bf16[1024,256]{1,0:T(8,128)(2,1)S(1)} %get-tuple-element.192, f32[1024]{0:T(1024)S(1)} %get-tuple-element.193, bf16[32768,256]{1,0:T(8,128)(2,1)} %get-tuple-element.191, s32[]{:T(128)S(6)} %select_n.43), kind=kOutput, calls=%fused_computation.3.clone.1 | convolution fusion | flops 2172648448 | bytes 2629636 | tf_op jit(solution)/shard_map/while/body/eval_jaxpr/dot_general | solution.py:27
  140.9 6.5 %fusion.11 = f32[1024]{0:T(1024)S(1)} fusion(bf16[1024,256]{1,0:T(8,128)(2,1)S(1)} %get-tuple-element.192, f32[1024]{0:T(1024)S(1)} %get-tuple-element.193, bf16[32768,256]{1,0:T(8,128)(2,1)} %get-tuple-element.191, s32[]{:T(128)S(6)} %select_n.43), kind=kOutput, calls=%fused_computation.3.clone.1 | convolution fusion | flops 2172648448 | bytes 2629636 | tf_op jit(solution)/shard_map/while/body/eval_jaxpr/dot_general | solution.py:27
  147.5 17.1 %psum.29 = f32[1024]{0:T(1024)S(1)} all-reduce(f32[1024]{0:T(1024)S(1)} %sub.59), channel_id=1, replica_groups=mesh['items'=8,'users'=4] {'items'}, use_global_device_ids=true, to_apply=%region_6.7 | all-reduce | flops 1024 | bytes 8192 | tf_op jit(solution)/shard_map/psum | solution.py:41
  164.7 1.3 divide_reduce_fusion.1
  166.0 6.3 %all-reduce = (f32[1]{0:T(128)}, f32[1]{0:T(128)}) all-reduce(f32[1]{0:T(128)} %bitcast.2, f32[1]{0:T(128)} %bitcast.1), channel_id=1, replica_groups=mesh['items'=8,'users'=4] {'users'}, use_global_device_ids=true, to_apply=%region_11.12 | all-reduce | flops 2 | bytes 16 | tf_op jit(solution)/shard_map/psum | solution.py:46
  172.3 1.8 %maximum_multiply_fusion = f32[2]{0:T(128)} fusion(f32[1]{0:T(128)} %get-tuple-element.137, f32[1]{0:T(128)} %get-tuple-element.138), kind=kLoop, calls=%fused_computation.22 | loop fusion | flops 4 | bytes 16 | tf_op jit(solution)/shard_map/div | solution.py:47
  (23 shorter events, 0.6 us)
Async XLA Ops:
  0.6 24.4 %copy-start.1 = (bf16[1024,32]{0,1:T(8,128)(2,1)S(1)}, bf16[1024,32]{0,1:T(8,128)(2,1)}, u32[]{:S(2)}) copy-start(bf16[1024,32]{0,1:T(8,128)(2,1)} %param.6) | copy-start | bytes 196612
  0.6 60.7 %copy-start.2 = (s32[1024]{0:T(1024)S(1)}, s32[1024]{0:T(1024)}, u32[]{:S(2)}) copy-start(s32[1024]{0:T(1024)} %param.8) | copy-start | bytes 12292
  94.8 69.9 %copy-start = (s32[1024,32]{0,1:T(8,128)S(1)}, s32[1024,32]{0,1:T(8,128)}, u32[]{:S(2)}) copy-start(s32[1024,32]{0,1:T(8,128)} %param.9) | copy-start | bytes 393220
where the time goes:
time: 175 us; the launch traced here: 174 us
  blocking collectives  78 us (45%)
  matrix products  52.4 us (30%)
  local copies, waits for them, and re-layouts  35.5 us (20%)
  other arithmetic  7.14 us (4%)
    dot_general x8, matrix products, add_block(): lax.dot_general(users, rows, (((1,), (1,)), ((), ())), preferred_element_...  52.4 us
    all_gather x1, blocking collectives, body(): users = lax.all_gather(user_emb, 'items', axis=1, tiled=True)  33 us
    gather x2, local copies, waits for them, and re-layouts, body(): hrows = item_emb[own_hist - start]  23 us
    psum x1, blocking collectives, body(): tscore = lax.psum(jnp.where(inside, partial_t, 0.0), 'items')  21.5 us
    psum x1, blocking collectives, body(): above = lax.psum(local, 'items') - correction  17.1 us
    gather x1, local copies, waits for them, and re-layouts, body(): own_rows = item_emb[jnp.clip(local_t, 0, item_dev - 1)]  11.4 us
    psum x1, blocking collectives, body(): hit_sum, gain_sum = lax.psum((jnp.sum(hit), jnp.sum(gain)), 'users')  6.3 us

commit v1 on v0

--- a/solution.py
+++ b/solution.py
@@ -15,7 +15,7 @@
     own_rows = item_emb[jnp.clip(local_t, 0, item_dev - 1)]
     users = lax.all_gather(user_emb, "items", axis=1, tiled=True)
     partial_t = jnp.sum(users.astype(jnp.float32) * own_rows.astype(jnp.float32), axis=1)
-    tscore = lax.psum(jnp.where(inside, partial_t, 0.0), "items")
+    tscore = jnp.sum(lax.all_gather(jnp.where(inside, partial_t, 0.0), "items"), axis=0)
     n_items = lax.axis_size("items")
     n_users = lax.axis_size("users")
     u_dev = users.shape[0]

time: 175 us -> 188 us (1.074)
  blocking collectives: 78 us -> 91.5 us
    all_gather x0 -> x1, blocking collectives: none -> 30.6 us  [body(): lax.all_gather(jnp.where(inside, partial_t, 0.0), 'items')]
    psum x1 -> x0, blocking collectives: 21.5 us -> none  [body(): tscore = lax.psum(jnp.where(inside, partial_t, 0.0), 'items')]
    psum x1, blocking collectives: 17.1 us -> 21.5 us  [body(): above = lax.psum(local, 'items') - correction]
where the time goes in v1:
time: 188 us
  blocking collectives  91.5 us (49%)
  matrix products  52.3 us (28%)
  local copies, waits for them, and re-layouts  35.5 us (19%)
  other arithmetic  7.15 us (4%)
    dot_general x8, matrix products, add_block(): lax.dot_general(users, rows, (((1,), (1,)), ((), ())), preferred_element_...  52.3 us
    all_gather x1, blocking collectives, body(): users = lax.all_gather(user_emb, 'items', axis=1, tiled=True)  33 us
    all_gather x1, blocking collectives, body(): lax.all_gather(jnp.where(inside, partial_t, 0.0), 'items')  30.6 us
    gather x2, local copies, waits for them, and re-layouts, body(): hrows = item_emb[own_hist - start]  23 us
    psum x1, blocking collectives, body(): above = lax.psum(local, 'items') - correction  21.5 us
    gather x1, local copies, waits for them, and re-layouts, body(): own_rows = item_emb[jnp.clip(local_t, 0, item_dev - 1)]  11.4 us
    psum x1, blocking collectives, body(): hit_sum, gain_sum = lax.psum((jnp.sum(hit), jnp.sum(gain)), 'users')  6.3 us

profile of v1, /device:TPU:0, one launch (start us, length us, event | category | flops | bytes accessed | tf_op | source)
XLA Modules:
  0.0 187.6 jit_solution(13013447190259843007)
XLA Ops:
  0.7 0.8 compare_select_fusion
  1.5 0.2 copy.14
  1.7 0.3 reshape.17
  2.0 20.9 %gather_fusion.1 = bf16[4096,256]{1,0:T(8,128)(2,1)S(1)} fusion(bf16[32768,256]{1,0:T(8,128)(2,1)} %param.7, s32[4096]{0:T(1024)S(1)} %broadcast_clamp_fusion), kind=kCustom, calls=%fused_computation.1 | custom fusion | bytes 4210688 | tf_op jit(solution)/shard_map/gather | solution.py:35
  22.9 2.1 %reshape.16 = bf16[1024,4,256]{2,1,0:T(4,128)(2,1)} reshape(bf16[4096,256]{1,0:T(8,128)(2,1)S(1)} %gather_fusion.1) | data formatting | bytes 4194304 | tf_op jit(solution)/shard_map/gather | solution.py:35
  25.0 33.0 %all_gather.9 = bf16[1024,256]{0,1:T(8,128)(2,1)S(1)} all-gather(bf16[1024,32]{0,1:T(8,128)(2,1)S(1)} %copy-done.1), channel_id=1, replica_groups=mesh['items'=8,'users'=4] {'items'}, dimensions={1}, use_global_device_ids=true | all-gather | bytes 589824 | tf_op jit(solution)/shard_map/all_gather | solution.py:16
  58.2 2.9 %multiply_reduce_fusion = f32[1024,4]{1,0:T(8,128)S(1)} fusion(f32[1024,256]{1,0:T(8,128)S(1)} %copy.20, bf16[1024,4,256]{2,1,0:T(4,128)(2,1)} %reshape.16), kind=kLoop, calls=%fused_computation.7 | loop fusion | flops 3141632 | bytes 3162112
  61.3 11.4 %gather_fusion = bf16[1024,256]{1,0:T(8,128)(2,1)S(1)} fusion(bf16[32768,256]{1,0:T(8,128)(2,1)} %param.7, s32[1024]{0:T(1024)S(1)} %fusion.4), kind=kCustom, calls=%fused_computation | custom fusion | bytes 1052672 | tf_op jit(solution)/shard_map/gather | solution.py:15
  72.7 0.2 copy.13
  73.0 0.2 multiply_reduce_fusion.1
  73.2 30.6 %all-gather = f32[8192]{0:T(1024)S(1)} all-gather(f32[1024]{0:T(1024)S(1)} %and_select_fusion), channel_id=2, replica_groups=mesh['items'=8,'users'=4] {'items'}, dimensions={0}, use_global_device_ids=true | all-gather | bytes 36864 | tf_op jit(solution)/shard_map/all_gather | solution.py:18
  103.9 52.7 %while.14 = (s32[]{:T(128)}, f32[1024]{0:T(1024)S(1)}, bf16[32768,256]{1,0:T(8,128)(2,1)}, bf16[1024,256]{1,0:T(8,128)(2,1)S(1)}, f32[1024]{0:T(1024)S(1)}, /*index=5*/s32[]{:T(128)}, s32[]{:T(128)}, s32[]{:T(128)}, s32[]{:T(128)}) while((s32[]{:T(128)}, f32[1024]{0:T(1024)S(1)}, bf16[32768,256]{1,0:T(8,128)(2,1)}, ...), condition=%wide.region_4.5_spmd.clone, body=%wide.region_2.4_spmd.clone.sunk | while | flops 2172650496 | bytes 2642073 | solution.py:32
  103.9 6.6 %fusion.11 = f32[1024]{0:T(1024)S(1)} fusion(bf16[1024,256]{1,0:T(8,128)(2,1)S(1)} %get-tuple-element.192, f32[1024]{0:T(1024)S(1)} %get-tuple-element.193, bf16[32768,256]{1,0:T(8,128)(2,1)} %get-tuple-element.191, s32[]{:T(128)S(6)} %select_n.43), kind=kOutput, calls=%fused_computation.3.clone.1 | convolution fusion | flops 2172648448 | bytes 2629636 | tf_op jit(solution)/shard_map/while/body/eval_jaxpr/dot_general | solution.py:27
  110.5 6.5 %fusion.11 = f32[1024]{0:T(1024)S(1)} fusion(bf16[1024,256]{1,0:T(8,128)(2,1)S(1)} %get-tuple-element.192, f32[1024]{0:T(1024)S(1)} %get-tuple-element.193, bf16[32768,256]{1,0:T(8,128)(2,1)} %get-tuple-element.191, s32[]{:T(128)S(6)} %select_n.43), kind=kOutput, calls=%fused_computation.3.clone.1 | convolution fusion | flops 2172648448 | bytes 2629636 | tf_op jit(solution)/shard_map/while/body/eval_jaxpr/dot_general | solution.py:27
  117.1 6.5 %fusion.11 = f32[1024]{0:T(1024)S(1)} fusion(bf16[1024,256]{1,0:T(8,128)(2,1)S(1)} %get-tuple-element.192, f32[1024]{0:T(1024)S(1)} %get-tuple-element.193, bf16[32768,256]{1,0:T(8,128)(2,1)} %get-tuple-element.191, s32[]{:T(128)S(6)} %select_n.43), kind=kOutput, calls=%fused_computation.3.clone.1 | convolution fusion | flops 2172648448 | bytes 2629636 | tf_op jit(solution)/shard_map/while/body/eval_jaxpr/dot_general | solution.py:27
  123.7 6.5 %fusion.11 = f32[1024]{0:T(1024)S(1)} fusion(bf16[1024,256]{1,0:T(8,128)(2,1)S(1)} %get-tuple-element.192, f32[1024]{0:T(1024)S(1)} %get-tuple-element.193, bf16[32768,256]{1,0:T(8,128)(2,1)} %get-tuple-element.191, s32[]{:T(128)S(6)} %select_n.43), kind=kOutput, calls=%fused_computation.3.clone.1 | convolution fusion | flops 2172648448 | bytes 2629636 | tf_op jit(solution)/shard_map/while/body/eval_jaxpr/dot_general | solution.py:27
  130.3 6.5 %fusion.11 = f32[1024]{0:T(1024)S(1)} fusion(bf16[1024,256]{1,0:T(8,128)(2,1)S(1)} %get-tuple-element.192, f32[1024]{0:T(1024)S(1)} %get-tuple-element.193, bf16[32768,256]{1,0:T(8,128)(2,1)} %get-tuple-element.191, s32[]{:T(128)S(6)} %select_n.43), kind=kOutput, calls=%fused_computation.3.clone.1 | convolution fusion | flops 2172648448 | bytes 2629636 | tf_op jit(solution)/shard_map/while/body/eval_jaxpr/dot_general | solution.py:27
  136.9 6.5 %fusion.11 = f32[1024]{0:T(1024)S(1)} fusion(bf16[1024,256]{1,0:T(8,128)(2,1)S(1)} %get-tuple-element.192, f32[1024]{0:T(1024)S(1)} %get-tuple-element.193, bf16[32768,256]{1,0:T(8,128)(2,1)} %get-tuple-element.191, s32[]{:T(128)S(6)} %select_n.43), kind=kOutput, calls=%fused_computation.3.clone.1 | convolution fusion | flops 2172648448 | bytes 2629636 | tf_op jit(solution)/shard_map/while/body/eval_jaxpr/dot_general | solution.py:27
  143.5 6.5 %fusion.11 = f32[1024]{0:T(1024)S(1)} fusion(bf16[1024,256]{1,0:T(8,128)(2,1)S(1)} %get-tuple-element.192, f32[1024]{0:T(1024)S(1)} %get-tuple-element.193, bf16[32768,256]{1,0:T(8,128)(2,1)} %get-tuple-element.191, s32[]{:T(128)S(6)} %select_n.43), kind=kOutput, calls=%fused_computation.3.clone.1 | convolution fusion | flops 2172648448 | bytes 2629636 | tf_op jit(solution)/shard_map/while/body/eval_jaxpr/dot_general | solution.py:27
  150.0 6.5 %fusion.11 = f32[1024]{0:T(1024)S(1)} fusion(bf16[1024,256]{1,0:T(8,128)(2,1)S(1)} %get-tuple-element.192, f32[1024]{0:T(1024)S(1)} %get-tuple-element.193, bf16[32768,256]{1,0:T(8,128)(2,1)} %get-tuple-element.191, s32[]{:T(128)S(6)} %select_n.43), kind=kOutput, calls=%fused_computation.3.clone.1 | convolution fusion | flops 2172648448 | bytes 2629636 | tf_op jit(solution)/shard_map/while/body/eval_jaxpr/dot_general | solution.py:27
  156.6 21.5 %psum.21 = f32[1024]{0:T(1024)S(1)} all-reduce(f32[1024]{0:T(1024)S(1)} %sub.59), channel_id=1, replica_groups=mesh['items'=8,'users'=4] {'items'}, use_global_device_ids=true, to_apply=%region_6.7 | all-reduce | flops 1024 | bytes 8192 | tf_op jit(solution)/shard_map/psum | solution.py:41
  178.2 1.3 divide_reduce_fusion.1
  179.5 6.3 %all-reduce = (f32[1]{0:T(128)}, f32[1]{0:T(128)}) all-reduce(f32[1]{0:T(128)} %bitcast.2, f32[1]{0:T(128)} %bitcast.1), channel_id=1, replica_groups=mesh['items'=8,'users'=4] {'users'}, use_global_device_ids=true, to_apply=%region_11.12 | all-reduce | flops 2 | bytes 16 | tf_op jit(solution)/shard_map/psum | solution.py:46
  185.8 1.8 maximum_multiply_fusion
  (25 shorter events, 0.6 us)
Async XLA Ops:
  0.6 24.4 %copy-start.1 = (bf16[1024,32]{0,1:T(8,128)(2,1)S(1)}, bf16[1024,32]{0,1:T(8,128)(2,1)}, u32[]{:S(2)}) copy-start(bf16[1024,32]{0,1:T(8,128)(2,1)} %param.6) | copy-start | bytes 196612
  0.6 60.7 %copy-start.2 = (s32[1024]{0:T(1024)S(1)}, s32[1024]{0:T(1024)}, u32[]{:S(2)}) copy-start(s32[1024]{0:T(1024)} %param.8) | copy-start | bytes 12292
  103.9 74.3 %copy-start = (s32[1024,32]{0,1:T(8,128)S(1)}, s32[1024,32]{0,1:T(8,128)}, u32[]{:S(2)}) copy-start(s32[1024,32]{0,1:T(8,128)} %param.9) | copy-start | bytes 393220
